TPU v7x, 32 devices: a whole 2x2x4 slice. The times are simulated.
32 devices in a mesh: py: 4 (over y, x), pz: 8 (over z, core).
Axes of the slice: x: 2, y: 2, z: 4, core: 2. Of those that a mesh axis runs over, the one named last changes fastest.
Arguments:
- species: float32 [4, 512, 64, 64], P(None, None, 'py', 'pz'), may hold values from -6 to 6
- coupling: float32 [4, 4], replicated, may hold values from -4 to 4
- symbol_x: float32 [512], replicated, may hold values from 0.3 to 3
- symbol_y: float32 [64], replicated, may hold values from 0.3 to 3
- symbol_z: float32 [64], replicated, may hold values from 0.3 to 3
Outputs:
- modes: float32 [4, 512, 64, 64], P(None, 'py', 'pz')
All inputs are finite; a program needn't handle non-finite values.
Results may differ from a plain program's by a relative error of at most 0.00007.
Values sent between devices are 32-bit elements; how exact they have to be, the bound alone decides.
A program may use at most 64 MiB of HBM per device.

v0:
```python
import functools

import jax
import jax.numpy as jnp
import numpy as np
from jax import lax
from jax.experimental import pallas as pl
from jax.experimental.pallas import tpu as pltpu
from jax.sharding import PartitionSpec as P

MESH = pl.DeviceIdType.MESH
F32 = jnp.float32
BF16 = jnp.bfloat16
LANES, SUBLANES = 128, 8
VMEM_BUDGET = 48 << 20


def mode_table(count):
    rank = jnp.arange(count)
    angle = (
        jnp.pi
        / (4 * count)
        * ((2 * rank[:, None] + 1) * (2 * rank[None, :] + 1) % (8 * count)).astype(jnp.float32)
    )
    return jnp.cos(angle) * (2.0 / count) ** 0.5


def transform_dim(values, dim):
    moved = jnp.tensordot(
        values, mode_table(values.shape[dim]), axes=([dim], [0]), precision=lax.Precision.HIGHEST
    )
    return jnp.moveaxis(moved, -1, dim)


def plain_shards(species, coupling, symbol_x, symbol_y, symbol_z):
    values = transform_dim(species, 1)
    values = lax.all_to_all(values, "py", split_axis=1, concat_axis=2, tiled=True)
    values = transform_dim(values, 2)
    values = lax.all_to_all(values, "pz", split_axis=2, concat_axis=3, tiled=True)
    values = transform_dim(values, 3)
    share_x = values.shape[1]
    part_x = lax.dynamic_slice_in_dim(symbol_x, lax.axis_index("py") * share_x, share_x)
    share_y = values.shape[2]
    part_y = lax.dynamic_slice_in_dim(symbol_y, lax.axis_index("pz") * share_y, share_y)
    symbol = part_x[:, None, None] + part_y[None, :, None] + symbol_z[None, None, :]
    weight = 1.0 / (1.0 + symbol)
    mixed = jnp.einsum("ab,bxyz->axyz", coupling, values, precision=lax.Precision.HIGHEST)
    return weight * values + (1.0 - weight) * mixed


def split_table(count):
    rank = 2 * np.arange(count) + 1
    table = np.cos(np.pi / (4 * count) * (rank[:, None] * rank[None, :] % (8 * count)))
    table = (table * np.sqrt(2.0 / count)).astype(np.float32)
    high = table.astype(BF16)
    low = (table - high.astype(np.float32)).astype(BF16)
    return np.stack([high, low])


def split(values):
    high = values.astype(BF16)
    low = (values - high.astype(F32)).astype(BF16)
    return high, low


def dot(a, b):
    return jnp.dot(a, b, preferred_element_type=F32)


def flipped(index, offset, count):
    if count & (count - 1):
        return lax.rem(index + offset, count)
    result = index
    bit = 1
    while bit < count:
        if offset & bit:
            result = result + bit - 2 * bit * lax.rem(index // bit, 2)
        bit *= 2
    return result


def source_of(index, offset, count):
    if count & (count - 1):
        return lax.rem(index + count - offset, count)
    return flipped(index, offset, count)


def kernel(
    dims, field_ref, hx_hbm, hy_hbm, hz_hbm, coupling_hbm, sx_hbm, sy_hbm, sz_hbm, out_ref,
    held, hx, hy, hz, coupling, sx, sy, sz, lines_out, lines, parts_out, parts, modes, weights,
    my, mz, load_sem, side_sem, send_y, recv_y, send_z, recv_z,
):
    fields, ny, nz, n_py, n_pz, yl, zl, share_x, share_y = dims
    py, pz = lax.axis_index("py"), lax.axis_index("pz")
    rows_y = yl * zl
    rows_z = share_y * zl
    depth_y = ny * zl
    rows_out = share_y * nz
    depth_z = n_pz * rows_z

    def load(f):
        return pltpu.make_async_copy(field_ref.at[f], held.at[f], load_sem.at[f])

    pairs = (
        (hx_hbm.at[0], hx.at[0]), (hx_hbm.at[1], hx.at[1]), (hy_hbm, hy), (hz_hbm, hz),
        (coupling_hbm, coupling), (sx_hbm, sx), (sy_hbm, sy), (sz_hbm, sz),
    )
    sides = [
        pltpu.make_async_copy(a, b, side_sem.at[i]) for i, (a, b) in enumerate(pairs)
    ]
    load(0).start()
    sides[0].start()
    sides[1].start()
    for f in range(1, fields):
        load(f).start()
    for side in sides[2:]:
        side.start()
    barrier = pltpu.get_barrier_semaphore()
    for o in range(1, n_pz):
        pl.semaphore_signal(
            barrier, inc=1, device_id={"pz": flipped(pz, o, n_pz)}, device_id_type=MESH
        )
    for o in range(1, n_py):
        pl.semaphore_signal(
            barrier, inc=1, device_id={"py": flipped(py, o, n_py)}, device_id_type=MESH
        )

    def copy_y(f, o):
        to = flipped(py, o, n_py)
        return pltpu.make_async_remote_copy(
            src_ref=lines_out.at[f, to],
            dst_ref=lines.at[f, pl.ds(py * rows_y, rows_y)],
            send_sem=send_y.at[f, o],
            recv_sem=recv_y.at[f, o],
            device_id={"py": to},
            device_id_type=MESH,
        )

    def copy_z(f, o):
        to = flipped(pz, o, n_pz)
        return pltpu.make_async_remote_copy(
            src_ref=parts_out.at[f, pl.ds(to * rows_z, rows_z)],
            dst_ref=parts.at[f, pl.ds(pz * rows_z, rows_z)],
            send_sem=send_z.at[f, o],
            recv_sem=recv_z.at[f, o],
            device_id={"pz": to},
            device_id_type=MESH,
        )

    for f in range(fields):
        load(f).wait()
        high, low = split(held[f])
        if f == 0:
            sides[0].wait()
            sides[1].wait()
        both = dot(jnp.concatenate([high, low], axis=0), hx[0])
        result = both[:rows_y] + both[rows_y:] + dot(high, hx[1])
        for d in range(n_py):
            lines_out[f, d] = result[:, d * share_x : (d + 1) * share_x]
        if f == 0:
            pl.semaphore_wait(barrier, n_py + n_pz - 2)
        for o in range(n_py - 1, 0, -1):
            copy_y(f, o).start()
        lines[f, pl.ds(py * rows_y, rows_y)] = lines_out[f, py]

    for side in sides[2:]:
        side.wait()

    def iota(shape, dim):
        return lax.broadcasted_iota(jnp.int32, shape, dim)

    row, col = iota((depth_y, ny), 0), iota((depth_y, ny), 1)
    pick = (row // zl == col).astype(F32).astype(BF16)
    row, col = iota((ny, depth_y), 0), iota((ny, depth_y), 1)
    spread = (col // zl == row).astype(F32).astype(BF16)
    row, col = iota((depth_y, depth_y), 0), iota((depth_y, depth_y), 1)
    keep = row % zl == col % zl
    for t in range(2):
        wide = dot(dot(pick, hy[t]).astype(BF16), spread)
        my[t] = jnp.where(keep, wide, 0.0).astype(BF16)
    def rows_transform(high_table, low_table, high, low):
        both = dot(high_table, jnp.concatenate([high, low], axis=1))
        return both[:, :share_x] + both[:, share_x:] + dot(low_table, high)

    halves = 2 if n_pz % 2 == 0 and n_pz & (n_pz - 1) == 0 else 1
    half_rows = depth_y // halves
    for f in range(fields):
        for o in range(n_py - 1, 0, -1):
            copy_y(f, o).wait_recv()
        high, low = split(lines[f])
        for h in range(halves):
            part = lax.rem(pz // (n_pz // halves) + h + 1, halves)
            span = pl.ds(pl.multiple_of(part * half_rows, half_rows), half_rows)
            parts_out[f, span] = rows_transform(my[0, span], my[1, span], high, low)
            top = n_pz - h * (n_pz // halves)
            for o in range(top - 1, max(top - n_pz // halves, 1) - 1, -1):
                copy_z(f, o).start()
        parts[f, pl.ds(pz * rows_z, rows_z)] = parts_out[f, pl.ds(pz * rows_z, rows_z)]

    row, col = iota((rows_out, nz), 0), iota((rows_out, nz), 1)
    pick = (row % nz == col).astype(F32).astype(BF16)
    row, col = iota((nz, depth_z), 0), iota((nz, depth_z), 1)
    spread = ((col // rows_z) * zl + col % zl == row).astype(F32).astype(BF16)
    row, col = iota((rows_out, depth_z), 0), iota((rows_out, depth_z), 1)
    keep = row // nz == (col // zl) % share_y
    for t in range(2):
        wide = dot(dot(pick, hz[t]).astype(BF16), spread)
        mz[t] = jnp.where(keep, wide, 0.0).astype(BF16)

    diagonal = iota((nz, nz), 0) == iota((nz, nz), 1)
    sz_column = jnp.sum(jnp.where(diagonal, sz[...], 0.0), axis=1, keepdims=True)
    sx_row = sx[:, pl.ds(pl.multiple_of(py * share_x, share_x), share_x)]
    for k in range(share_y):
        symbol = (sx_row + sy[pz * share_y + k]) + sz_column
        weights[pl.ds(k * nz, nz)] = 1.0 / (1.0 + symbol)

    last = fields - 1
    for f in range(fields):
        for o in range(n_pz - 1, 0, -1):
            copy_z(f, o).wait_recv()
        high, low = split(parts[f])
        if f < last:
            modes[f] = rows_transform(mz[0], mz[1], high, low)
        if f == last - 1:
            for k in range(share_y):
                span = pl.ds(k * nz, nz)
                weight = weights[span]
                old = [modes[b, span] for b in range(last)]
                for a in range(fields):
                    mixed = coupling[a, 0] * old[0]
                    for b in range(1, last):
                        mixed = mixed + coupling[a, b] * old[b]
                    mixed = (1.0 - weight) * mixed
                    out_ref[a, span] = mixed + weight * old[a] if a < last else mixed
        if f == last:
            result = rows_transform(mz[0], mz[1], high, low)
            weight = weights[...]
            rest = (1.0 - weight) * result
            for a in range(fields):
                new = out_ref[a] + coupling[a, last] * rest
                out_ref[a] = new + weight * result if a == last else new
    for f in range(fields):
        for o in range(1, n_py):
            copy_y(f, o).wait_send()
        for o in range(1, n_pz):
            copy_z(f, o).wait_send()


def shards(n_py, n_pz, species, coupling, symbol_x, symbol_y, symbol_z):
    fields, nx, yl, zl = species.shape
    ny, nz = yl * n_py, zl * n_pz
    share_x, share_y = nx // n_py, ny // n_pz
    block = fields * nx * yl * zl
    tables = 2 * (nx * nx + (ny * zl) ** 2 + (share_y * nz) ** 2)
    need = 7 * 4 * block + 2 * tables + 16 * max(ny * zl, share_y * nz) ** 2
    if share_x % LANES or zl % SUBLANES or nx % n_py or ny % n_pz or need > VMEM_BUDGET or fields < 2:
        return plain_shards(species, coupling, symbol_x, symbol_y, symbol_z)
    dims = (fields, ny, nz, n_py, n_pz, yl, zl, share_x, share_y)
    rows_y, depth_y, depth_z = yl * zl, ny * zl, share_y * nz
    vmem = pl.BlockSpec(memory_space=pltpu.VMEM)
    hbm = pl.BlockSpec(memory_space=pltpu.HBM)
    values = jnp.transpose(species, (0, 2, 3, 1)).reshape(fields, rows_y, nx)
    out = pl.pallas_call(
        functools.partial(kernel, dims),
        out_shape=jax.ShapeDtypeStruct((fields, depth_z, share_x), F32),
        in_specs=[hbm] * 8,
        out_specs=vmem,
        scratch_shapes=[
            pltpu.VMEM((fields, rows_y, nx), F32),
            pltpu.VMEM((2, nx, nx), BF16),
            pltpu.VMEM((2, ny, ny), BF16),
            pltpu.VMEM((2, nz, nz), BF16),
            pltpu.SMEM((fields, fields), F32),
            pltpu.VMEM((1, nx), F32),
            pltpu.SMEM((ny,), F32),
            pltpu.VMEM((1, nz), F32),
            pltpu.VMEM((fields, n_py, rows_y, share_x), F32),
            pltpu.VMEM((fields, depth_y, share_x), F32),
            pltpu.VMEM((fields, depth_y, share_x), F32),
            pltpu.VMEM((fields, depth_z, share_x), F32),
            pltpu.VMEM((fields - 1, depth_z, share_x), F32),
            pltpu.VMEM((depth_z, share_x), F32),
            pltpu.VMEM((2, depth_y, depth_y), BF16),
            pltpu.VMEM((2, depth_z, depth_z), BF16),
            pltpu.SemaphoreType.DMA((fields,)),
            pltpu.SemaphoreType.DMA((8,)),
            pltpu.SemaphoreType.DMA((fields, n_py)),
            pltpu.SemaphoreType.DMA((fields, n_py)),
            pltpu.SemaphoreType.DMA((fields, n_pz)),
            pltpu.SemaphoreType.DMA((fields, n_pz)),
        ],
        compiler_params=pltpu.CompilerParams(
            collective_id=0, has_side_effects=True, vmem_limit_bytes=54500000
        ),
    )(
        values,
        jnp.asarray(split_table(nx)),
        jnp.asarray(split_table(ny)),
        jnp.asarray(split_table(nz)),
        coupling,
        symbol_x.reshape(1, nx),
        symbol_y,
        symbol_z.reshape(1, nz),
    )
    return jnp.transpose(out.reshape(fields, share_y, nz, share_x), (0, 3, 1, 2))


def solution(mesh):
    return jax.shard_map(
        functools.partial(shards, mesh.shape["py"], mesh.shape["pz"]),
        mesh=mesh,
        in_specs=(P(None, None, "py", "pz"), P(), P(), P(), P()),
        out_specs=P(None, "py", "pz", None),
        check_vma=False,
    )
```

profile of v0, /device:TPU:0, one launch (start us, length us, event | category | flops | bytes accessed | tf_op | source)
XLA Modules:
  0.0 38.0 jit_solution(13674102365229037284)
XLA Ops:
  0.0 0.0 copy-start.2
  0.0 0.0 copy-start.1
  0.0 0.0 copy-start.3
  0.0 0.0 copy-start.4
  0.0 0.7 %copy-done.2 = f32[512]{0:T(512)S(1)} copy-done((f32[512]{0:T(512)S(1)}, f32[512]{0:T(512)}, u32[]{:S(2)}) %copy-start.2) | copy-done | bytes 2072
  0.7 0.0 copy-done.1
  0.7 0.0 copy-done.3
  0.7 0.0 copy-done.4
  0.7 0.0 copy-start
  0.7 0.8 %copy-done = bf16[2,64,64]{2,1,0:T(8,128)(2,1)S(1)} copy-done((bf16[2,64,64]{2,1,0:T(8,128)(2,1)S(1)}, bf16[2,64,64]{2,1,0:T(8,128)(2,1)}, u32[]{:S(2)}) %copy-start) | copy-done | bytes 16408
  1.5 35.6 %shard_map.82 = f32[4,512,128]{2,1,0:T(8,128)S(1)} custom-call(f32[4,128,512]{2,1,0:T(8,128)} %bitcast.11, bf16[2,512,512]{2,1,0:T(8,128)(2,1)} %constant.4.clone.hx_hbm, bf16[2,64,64]{2,1,0:T(8,128)(2,1)S(1)} %copy-done, bf16[2,64,64]{2,1,0:T(8,128)(2,1)S(1)} %copy-done, f32[4,4]{1,0:T(4,128)S(1)} %copy-done.1, f32[1,512]{1,0:T(1,128)S(1)} %bitcast.9, ...), custom_call_target="tpu_custom_call" | custom-call | tf_op jit(solution)/shard_map/pallas_call | solution.py:263
  37.0 1.0 %copy.10 = f32[4,128,8,64]{1,3,2,0:T(8,128)} copy(f32[4,128,8,64]{1,3,2,0:T(8,128)S(1)} %bitcast.8) | data formatting | bytes 2097152
Async XLA Ops:
  0.0 0.7 %copy-start.2 = (f32[512]{0:T(512)S(1)}, f32[512]{0:T(512)}, u32[]{:S(2)}) copy-start(f32[512]{0:T(512)} %param.10) | copy-start | bytes 6148
  0.0 0.7 %copy-start.1 = (f32[4,4]{1,0:T(4,128)S(1)}, f32[4,4]{1,0:T(4,128)}, u32[]{:S(2)}) copy-start(f32[4,4]{1,0:T(4,128)} %coupling_hbm.1) | copy-start | bytes 196
  0.0 0.7 %copy-start.3 = (f32[64]{0:T(128)S(1)}, f32[64]{0:T(128)}, u32[]{:S(2)}) copy-start(f32[64]{0:T(128)} %sy_hbm.1) | copy-start | bytes 772
  0.0 0.7 %copy-start.4 = (f32[64]{0:T(128)S(1)}, f32[64]{0:T(128)}, u32[]{:S(2)}) copy-start(f32[64]{0:T(128)} %param.12) | copy-start | bytes 772
  0.7 0.8 %copy-start = (bf16[2,64,64]{2,1,0:T(8,128)(2,1)S(1)}, bf16[2,64,64]{2,1,0:T(8,128)(2,1)}, u32[]{:S(2)}) copy-start(bf16[2,64,64]{2,1,0:T(8,128)(2,1)} %constant.5.clone.hy_hbm.hz_hbm) | copy-start | bytes 49156
where the time goes:
time: 38.2 us; the launch traced here: 38 us
  Pallas kernels  35.6 us (93%)
  local copies, waits for them, and re-layouts  2.43 us (6%)
    pallas_call x1, Pallas kernels, shards(): pl.pallas_call(functools.partial(kernel, dims), out_shape=jax.ShapeDtypeS...  35.6 us
    unnamed x11, local copies, waits for them, and re-layouts  2.43 us

commit v1 on v0

--- a/solution.py
+++ b/solution.py
@@ -293,14 +293,19 @@
             collective_id=0, has_side_effects=True, vmem_limit_bytes=54500000
         ),
     )(
-        values,
-        jnp.asarray(split_table(nx)),
-        jnp.asarray(split_table(ny)),
-        jnp.asarray(split_table(nz)),
-        coupling,
-        symbol_x.reshape(1, nx),
-        symbol_y,
-        symbol_z.reshape(1, nz),
+        *(
+            pltpu.with_memory_space_constraint(x, pltpu.HBM)
+            for x in (
+                values,
+                jnp.asarray(split_table(nx)),
+                jnp.asarray(split_table(ny)),
+                jnp.asarray(split_table(nz)),
+                coupling,
+                symbol_x.reshape(1, nx),
+                symbol_y,
+                symbol_z.reshape(1, nz),
+            )
+        )
     )
     return jnp.transpose(out.reshape(fields, share_y, nz, share_x), (0, 3, 1, 2))
 

time: 38.2 us -> 36.7 us (0.961)
  local copies, waits for them, and re-layouts: 2.43 us -> 0.97 us
    unnamed x11 -> x1, local copies, waits for them, and re-layouts: 2.43 us -> 0.97 us
where the time goes in v1:
time: 36.7 us; the launch traced here: 36.5 us
  Pallas kernels  35.5 us (97%)
  local copies, waits for them, and re-layouts  0.97 us (3%)
    pallas_call x1, Pallas kernels, shards(): pl.pallas_call(functools.partial(kernel, dims), out_shape=jax.ShapeDtypeS...  35.5 us
    unnamed x1, local copies, waits for them, and re-layouts  0.97 us

profile of v1, /device:TPU:0, one launch (start us, length us, event | category | flops | bytes accessed | tf_op | source)
XLA Modules:
  0.0 36.5 jit_solution(9502018758440580456)
XLA Ops:
  0.0 35.5 %shard_map.82 = f32[4,512,128]{2,1,0:T(8,128)S(1)} custom-call(f32[4,128,512]{2,1,0:T(8,128)} %bitcast.9, bf16[2,512,512]{2,1,0:T(8,128)(2,1)} %constant.4.clone.hx_hbm, bf16[2,64,64]{2,1,0:T(8,128)(2,1)} %constant.5.clone.hy_hbm.hz_hbm, bf16[2,64,64]{2,1,0:T(8,128)(2,1)} %constant.5.clone.hy_hbm.hz_hbm, f32[4,4]{1,0:T(4,128)} %coupling_hbm.1, ...), custom_call_target="tpu_custom_call" | custom-call | tf_op jit(solution)/shard_map/pallas_call | solution.py:263
  35.5 1.0 %copy.10 = f32[4,128,8,64]{1,3,2,0:T(8,128)} copy(f32[4,128,8,64]{1,3,2,0:T(8,128)S(1)} %bitcast.8) | data formatting | bytes 2097152

commit v2 on v1

--- a/solution.py
+++ b/solution.py
@@ -88,7 +88,8 @@
 def kernel(
     dims, field_ref, hx_hbm, hy_hbm, hz_hbm, coupling_hbm, sx_hbm, sy_hbm, sz_hbm, out_ref,
     held, hx, hy, hz, coupling, sx, sy, sz, lines_out, lines, parts_out, parts, modes, weights,
-    my, mz, load_sem, side_sem, send_y, recv_y, send_z, recv_z,
+    my, mz, far, far_lines, far_out, load_sem, side_sem, send_y, recv_y, send_z, recv_z,
+    send_raw, recv_raw, send_relay, recv_relay, send_far, recv_far,
 ):
     fields, ny, nz, n_py, n_pz, yl, zl, share_x, share_y = dims
     py, pz = lax.axis_index("py"), lax.axis_index("pz")
@@ -108,6 +109,15 @@
     sides = [
         pltpu.make_async_copy(a, b, side_sem.at[i]) for i, (a, b) in enumerate(pairs)
     ]
+    barrier = pltpu.get_barrier_semaphore()
+    for o in range(n_pz - 1, 0, -1):
+        pl.semaphore_signal(
+            barrier, inc=1, device_id={"pz": flipped(pz, o, n_pz)}, device_id_type=MESH
+        )
+    for o in range(n_py - 1, 0, -1):
+        pl.semaphore_signal(
+            barrier, inc=1, device_id={"py": flipped(py, o, n_py)}, device_id_type=MESH
+        )
     load(0).start()
     sides[0].start()
     sides[1].start()
@@ -115,15 +125,6 @@
         load(f).start()
     for side in sides[2:]:
         side.start()
-    barrier = pltpu.get_barrier_semaphore()
-    for o in range(1, n_pz):
-        pl.semaphore_signal(
-            barrier, inc=1, device_id={"pz": flipped(pz, o, n_pz)}, device_id_type=MESH
-        )
-    for o in range(1, n_py):
-        pl.semaphore_signal(
-            barrier, inc=1, device_id={"py": flipped(py, o, n_py)}, device_id_type=MESH
-        )
 
     def copy_y(f, o):
         to = flipped(py, o, n_py)
@@ -136,13 +137,66 @@
             device_id_type=MESH,
         )
 
-    def copy_z(f, o):
+    near = n_pz // 2
+    half = pz // near
+
+    def across(j):
+        return (1 - half) * (n_pz - 1 - j) + half * j
+
+    def beside(o):
+        return flipped(pz, o, n_pz)
+
+    def copy_z(f, peer):
+        return pltpu.make_async_remote_copy(
+            src_ref=parts_out.at[f, pl.ds(peer * rows_z, rows_z)],
+            dst_ref=parts.at[f, pl.ds(pz * rows_z, rows_z)],
+            send_sem=send_z.at[f, peer],
+            recv_sem=recv_z.at[f, pz],
+            device_id={"pz": peer},
+            device_id_type=MESH,
+        )
+
+    def arrival_z(f, peer):
+        return pltpu.make_async_remote_copy(
+            src_ref=parts_out.at[f, pl.ds(peer * rows_z, rows_z)],
+            dst_ref=parts.at[f, pl.ds(peer * rows_z, rows_z)],
+            send_sem=send_z.at[f, peer],
+            recv_sem=recv_z.at[f, peer],
+            device_id={"pz": peer},
+            device_id_type=MESH,
+        )
+
+    mirror = flipped(pz, near, n_pz)
+    raw_role = lax.rem(pz, 2) == 0
+    plain_role = jnp.logical_not(raw_role)
+
+    raw = pltpu.make_async_remote_copy(
+        src_ref=lines_out.at[0],
+        dst_ref=far,
+        send_sem=send_raw.at[0],
+        recv_sem=recv_raw.at[0],
+        device_id={"pz": mirror},
+        device_id_type=MESH,
+    )
+
+    def copy_relay(o):
+        to = flipped(py, o, n_py)
+        return pltpu.make_async_remote_copy(
+            src_ref=far.at[to],
+            dst_ref=far_lines.at[pl.ds(py * rows_y, rows_y)],
+            send_sem=send_relay.at[o],
+            recv_sem=recv_relay.at[o],
+            device_id={"py": to},
+            device_id_type=MESH,
+        )
+
+    def copy_far(o):
         to = flipped(pz, o, n_pz)
         return pltpu.make_async_remote_copy(
-            src_ref=parts_out.at[f, pl.ds(to * rows_z, rows_z)],
-            dst_ref=parts.at[f, pl.ds(pz * rows_z, rows_z)],
-            send_sem=send_z.at[f, o],
-            recv_sem=recv_z.at[f, o],
+            src_ref=far_out.at[pl.ds((to - half * near) * rows_z, rows_z)],
+            dst_ref=parts.at[0, pl.ds(mirror * rows_z, rows_z)],
+            send_sem=send_far.at[o],
+            recv_sem=recv_far.at[o],
             device_id={"pz": to},
             device_id_type=MESH,
         )
@@ -157,10 +211,18 @@
         result = both[:rows_y] + both[rows_y:] + dot(high, hx[1])
         for d in range(n_py):
             lines_out[f, d] = result[:, d * share_x : (d + 1) * share_x]
+        def send_lines(f):
+            for o in range(n_py - 1, 0, -1):
+                copy_y(f, o).start()
+
         if f == 0:
             pl.semaphore_wait(barrier, n_py + n_pz - 2)
-        for o in range(n_py - 1, 0, -1):
-            copy_y(f, o).start()
+            pl.when(raw_role)(raw.start)
+            pl.when(plain_role)(functools.partial(send_lines, 0))
+        else:
+            send_lines(f)
+        if f == 1:
+            pl.when(raw_role)(functools.partial(send_lines, 0))
         lines[f, pl.ds(py * rows_y, rows_y)] = lines_out[f, py]
 
     for side in sides[2:]:
@@ -182,20 +244,66 @@
         both = dot(high_table, jnp.concatenate([high, low], axis=1))
         return both[:, :share_x] + both[:, share_x:] + dot(low_table, high)
 
-    halves = 2 if n_pz % 2 == 0 and n_pz & (n_pz - 1) == 0 else 1
-    half_rows = depth_y // halves
-    for f in range(fields):
+    half_rows = depth_y // 2
+
+    def send_second(f):
+        for j in range(near // 2, near):
+            copy_z(f, across(j)).start()
+
+    def y_step(f, before):
         for o in range(n_py - 1, 0, -1):
             copy_y(f, o).wait_recv()
         high, low = split(lines[f])
-        for h in range(halves):
-            part = lax.rem(pz // (n_pz // halves) + h + 1, halves)
+        for h in range(2):
+            part = lax.rem(half + h + 1, 2)
             span = pl.ds(pl.multiple_of(part * half_rows, half_rows), half_rows)
             parts_out[f, span] = rows_transform(my[0, span], my[1, span], high, low)
-            top = n_pz - h * (n_pz // halves)
-            for o in range(top - 1, max(top - n_pz // halves, 1) - 1, -1):
-                copy_z(f, o).start()
+            if h == 0:
+                for j in range(near // 2):
+                    copy_z(f, across(j)).start()
+                if before is not None:
+                    send_second(before)
+                if f == fields - 1:
+                    send_second(f)
+            else:
+                for o in range(near - 1, 0, -1):
+                    copy_z(f, beside(o)).start()
         parts[f, pl.ds(pz * rows_z, rows_z)] = parts_out[f, pl.ds(pz * rows_z, rows_z)]
+
+    def relay():
+        raw.wait_recv()
+        for o in range(n_py - 1, 0, -1):
+            copy_relay(o).start()
+        far_lines[pl.ds(py * rows_y, rows_y)] = far[py]
+
+    def near_step():
+        for o in range(n_py - 1, 0, -1):
+            copy_y(0, o).wait_recv()
+        span = pl.ds(pl.multiple_of(half * half_rows, half_rows), half_rows)
+        high, low = split(lines[0])
+        parts_out[0, span] = rows_transform(my[0, span], my[1, span], high, low)
+        for o in range(near - 1, 0, -1):
+            copy_z(0, beside(o)).start()
+        parts[0, pl.ds(pz * rows_z, rows_z)] = parts_out[0, pl.ds(pz * rows_z, rows_z)]
+        for o in range(n_py - 1, 0, -1):
+            copy_relay(o).wait_recv()
+        high, low = split(far_lines[...])
+        far_out[...] = rows_transform(my[0, span], my[1, span], high, low)
+        for o in range(near - 1, 0, -1):
+            copy_far(o).start()
+        parts[0, pl.ds(mirror * rows_z, rows_z)] = far_out[
+            pl.ds((pz - half * near) * rows_z, rows_z)
+        ]
+
+    pl.when(plain_role)(functools.partial(y_step, 0, None))
+    for f in range(1, fields):
+        if f == fields - 1:
+            pl.when(raw_role)(near_step)
+        if f == 1:
+            pl.when(plain_role)(functools.partial(send_second, 0))
+        y_step(f, f - 1 if f > 1 else None)
+        if f == 1:
+            pl.when(raw_role)(relay)
 
     row, col = iota((rows_out, nz), 0), iota((rows_out, nz), 1)
     pick = (row % nz == col).astype(F32).astype(BF16)
@@ -214,14 +322,25 @@
         symbol = (sx_row + sy[pz * share_y + k]) + sz_column
         weights[pl.ds(k * nz, nz)] = 1.0 / (1.0 + symbol)
 
+    def wait_first(role):
+        for o in range(1, n_pz):
+            if o % 2 == 1 - role or o < near:
+                arrival_z(0, beside(o)).wait_recv()
+            if o % 2 == role and o < near:
+                copy_far(o).wait_recv()
+
     last = fields - 1
-    for f in range(fields):
-        for o in range(n_pz - 1, 0, -1):
-            copy_z(f, o).wait_recv()
+    for f in [*range(1, last), 0, last]:
+        if f == 0:
+            pl.when(raw_role)(functools.partial(wait_first, 0))
+            pl.when(plain_role)(functools.partial(wait_first, 1))
+        else:
+            for o in range(1, n_pz):
+                arrival_z(f, beside(o)).wait_recv()
         high, low = split(parts[f])
         if f < last:
             modes[f] = rows_transform(mz[0], mz[1], high, low)
-        if f == last - 1:
+        if f == 0:
             for k in range(share_y):
                 span = pl.ds(k * nz, nz)
                 weight = weights[span]
@@ -243,7 +362,21 @@
         for o in range(1, n_py):
             copy_y(f, o).wait_send()
         for o in range(1, n_pz):
-            copy_z(f, o).wait_send()
+            if f or o < near:
+                copy_z(f, beside(o)).wait_send()
+
+    @pl.when(raw_role)
+    def _():
+        raw.wait_send()
+        for o in range(1, n_py):
+            copy_relay(o).wait_send()
+        for o in range(1, near):
+            copy_far(o).wait_send()
+
+    @pl.when(plain_role)
+    def _():
+        for o in range(near, n_pz):
+            copy_z(0, beside(o)).wait_send()
 
 
 def shards(n_py, n_pz, species, coupling, symbol_x, symbol_y, symbol_z):
@@ -253,7 +386,8 @@
     block = fields * nx * yl * zl
     tables = 2 * (nx * nx + (ny * zl) ** 2 + (share_y * nz) ** 2)
     need = 7 * 4 * block + 2 * tables + 16 * max(ny * zl, share_y * nz) ** 2
-    if share_x % LANES or zl % SUBLANES or nx % n_py or ny % n_pz or need > VMEM_BUDGET or fields < 2:
+    bad = share_x % LANES or zl % SUBLANES or nx % n_py or ny % n_pz
+    if bad or need > VMEM_BUDGET or fields < 3 or n_pz % 4 or n_pz & (n_pz - 1):
         return plain_shards(species, coupling, symbol_x, symbol_y, symbol_z)
     dims = (fields, ny, nz, n_py, n_pz, yl, zl, share_x, share_y)
     rows_y, depth_y, depth_z = yl * zl, ny * zl, share_y * nz
@@ -282,12 +416,21 @@
             pltpu.VMEM((depth_z, share_x), F32),
             pltpu.VMEM((2, depth_y, depth_y), BF16),
             pltpu.VMEM((2, depth_z, depth_z), BF16),
+            pltpu.VMEM((n_py, rows_y, share_x), F32),
+            pltpu.VMEM((depth_y, share_x), F32),
+            pltpu.VMEM((depth_y // 2, share_x), F32),
             pltpu.SemaphoreType.DMA((fields,)),
             pltpu.SemaphoreType.DMA((8,)),
             pltpu.SemaphoreType.DMA((fields, n_py)),
             pltpu.SemaphoreType.DMA((fields, n_py)),
             pltpu.SemaphoreType.DMA((fields, n_pz)),
             pltpu.SemaphoreType.DMA((fields, n_pz)),
+            pltpu.SemaphoreType.DMA((1,)),
+            pltpu.SemaphoreType.DMA((1,)),
+            pltpu.SemaphoreType.DMA((n_py,)),
+            pltpu.SemaphoreType.DMA((n_py,)),
+            pltpu.SemaphoreType.DMA((n_pz // 2,)),
+            pltpu.SemaphoreType.DMA((n_pz // 2,)),
         ],
         compiler_params=pltpu.CompilerParams(
             collective_id=0, has_side_effects=True, vmem_limit_bytes=54500000

time: 36.7 us -> 34 us (0.926)
  the two profiles are of different devices: /device:TPU:0 before, /device:TPU:9 now
where the time goes in v2:
time: 34 us; the launch traced here: 33.8 us
  Pallas kernels  32.9 us (97%)
  local copies, waits for them, and re-layouts  0.97 us (3%)
    pallas_call x1, Pallas kernels, shards(): pl.pallas_call(functools.partial(kernel, dims), out_shape=jax.ShapeDtypeS...  32.9 us
    unnamed x1, local copies, waits for them, and re-layouts  0.97 us

profile of v2, /device:TPU:9, one launch (start us, length us, event | category | flops | bytes accessed | tf_op | source)
XLA Modules:
  0.0 33.8 jit_solution(11406204175274698848)
XLA Ops:
  0.0 32.9 %shard_map.82 = f32[4,512,128]{2,1,0:T(8,128)S(1)} custom-call(f32[4,128,512]{2,1,0:T(8,128)} %bitcast.9, bf16[2,512,512]{2,1,0:T(8,128)(2,1)} %constant.4.clone.hx_hbm, bf16[2,64,64]{2,1,0:T(8,128)(2,1)} %constant.5.clone.hy_hbm.hz_hbm, bf16[2,64,64]{2,1,0:T(8,128)(2,1)} %constant.5.clone.hy_hbm.hz_hbm, f32[4,4]{1,0:T(4,128)} %coupling_hbm.1, ...), custom_call_target="tpu_custom_call" | custom-call | tf_op jit(solution)/shard_map/pallas_call | solution.py:397
  32.9 1.0 %copy.10 = f32[4,128,8,64]{1,3,2,0:T(8,128)} copy(f32[4,128,8,64]{1,3,2,0:T(8,128)S(1)} %bitcast.8) | data formatting | bytes 2097152

commit v3 on v2

--- a/solution.py
+++ b/solution.py
@@ -89,21 +89,22 @@
     dims, field_ref, hx_hbm, hy_hbm, hz_hbm, coupling_hbm, sx_hbm, sy_hbm, sz_hbm, out_ref,
     held, hx, hy, hz, coupling, sx, sy, sz, lines_out, lines, parts_out, parts, modes, weights,
     my, mz, far, far_lines, far_out, load_sem, side_sem, send_y, recv_y, send_z, recv_z,
-    send_raw, recv_raw, send_relay, recv_relay, send_far, recv_far,
+    send_raw, recv_raw, send_relay, recv_relay, send_far,
 ):
     fields, ny, nz, n_py, n_pz, yl, zl, share_x, share_y = dims
     py, pz = lax.axis_index("py"), lax.axis_index("pz")
     rows_y = yl * zl
     rows_z = share_y * zl
     depth_y = ny * zl
-    rows_out = share_y * nz
-    depth_z = n_pz * rows_z
+    group = max(g for g in range(1, share_y + 1) if share_y % g == 0 and g * nz <= max(nz, 256))
+    rows_g, rows_out = group * zl, group * nz
+    depth_g = n_pz * rows_g
 
     def load(f):
         return pltpu.make_async_copy(field_ref.at[f], held.at[f], load_sem.at[f])
 
     pairs = (
-        (hx_hbm.at[0], hx.at[0]), (hx_hbm.at[1], hx.at[1]), (hy_hbm, hy), (hz_hbm, hz),
+        (hx_hbm, hx), (hy_hbm, hy), (hz_hbm, hz),
         (coupling_hbm, coupling), (sx_hbm, sx), (sy_hbm, sy), (sz_hbm, sz),
     )
     sides = [
@@ -120,10 +121,9 @@
         )
     load(0).start()
     sides[0].start()
-    sides[1].start()
     for f in range(1, fields):
         load(f).start()
-    for side in sides[2:]:
+    for side in sides[1:]:
         side.start()
 
     def copy_y(f, o):
@@ -131,8 +131,8 @@
         return pltpu.make_async_remote_copy(
             src_ref=lines_out.at[f, to],
             dst_ref=lines.at[f, pl.ds(py * rows_y, rows_y)],
-            send_sem=send_y.at[f, o],
-            recv_sem=recv_y.at[f, o],
+            send_sem=send_y.at[f],
+            recv_sem=recv_y.at[f],
             device_id={"py": to},
             device_id_type=MESH,
         )
@@ -146,25 +146,22 @@
     def beside(o):
         return flipped(pz, o, n_pz)
 
-    def copy_z(f, peer):
+    def copy_z(f, peer, piece=None):
+        rows, first = (rows_z, 0) if piece is None else (rows_g, piece * rows_g)
         return pltpu.make_async_remote_copy(
-            src_ref=parts_out.at[f, pl.ds(peer * rows_z, rows_z)],
-            dst_ref=parts.at[f, pl.ds(pz * rows_z, rows_z)],
-            send_sem=send_z.at[f, peer],
-            recv_sem=recv_z.at[f, pz],
+            src_ref=parts_out.at[f, pl.ds(peer * rows_z + first, rows)],
+            dst_ref=parts.at[f, pl.ds(pz * rows_z + first, rows)],
+            send_sem=send_z.at[f],
+            recv_sem=recv_z.at[f if piece is None else f + piece],
             device_id={"pz": peer},
             device_id_type=MESH,
         )
 
-    def arrival_z(f, peer):
-        return pltpu.make_async_remote_copy(
-            src_ref=parts_out.at[f, pl.ds(peer * rows_z, rows_z)],
-            dst_ref=parts.at[f, pl.ds(peer * rows_z, rows_z)],
-            send_sem=send_z.at[f, peer],
-            recv_sem=recv_z.at[f, peer],
-            device_id={"pz": peer},
-            device_id_type=MESH,
-        )
+    def wait_for(ref, sem):
+        pltpu.make_async_copy(ref, ref, sem).wait()
+
+    def wait_lines(f):
+        wait_for(lines.at[f, pl.ds(0, (n_py - 1) * rows_y)], recv_y.at[f])
 
     mirror = flipped(pz, near, n_pz)
     raw_role = lax.rem(pz, 2) == 0
@@ -184,8 +181,8 @@
         return pltpu.make_async_remote_copy(
             src_ref=far.at[to],
             dst_ref=far_lines.at[pl.ds(py * rows_y, rows_y)],
-            send_sem=send_relay.at[o],
-            recv_sem=recv_relay.at[o],
+            send_sem=send_relay.at[0],
+            recv_sem=recv_relay.at[0],
             device_id={"py": to},
             device_id_type=MESH,
         )
@@ -195,8 +192,8 @@
         return pltpu.make_async_remote_copy(
             src_ref=far_out.at[pl.ds((to - half * near) * rows_z, rows_z)],
             dst_ref=parts.at[0, pl.ds(mirror * rows_z, rows_z)],
-            send_sem=send_far.at[o],
-            recv_sem=recv_far.at[o],
+            send_sem=send_far.at[0],
+            recv_sem=recv_z.at[0],
             device_id={"pz": to},
             device_id_type=MESH,
         )
@@ -206,7 +203,6 @@
         high, low = split(held[f])
         if f == 0:
             sides[0].wait()
-            sides[1].wait()
         both = dot(jnp.concatenate([high, low], axis=0), hx[0])
         result = both[:rows_y] + both[rows_y:] + dot(high, hx[1])
         for d in range(n_py):
@@ -225,7 +221,7 @@
             pl.when(raw_role)(functools.partial(send_lines, 0))
         lines[f, pl.ds(py * rows_y, rows_y)] = lines_out[f, py]
 
-    for side in sides[2:]:
+    for side in sides[1:]:
         side.wait()
 
     def iota(shape, dim):
@@ -246,28 +242,33 @@
 
     half_rows = depth_y // 2
 
-    def send_second(f):
-        for j in range(near // 2, near):
-            copy_z(f, across(j)).start()
+    last = fields - 1
+    pieces = share_y // group
+
+    def send_parts(f, peers):
+        for piece in range(pieces) if f == last else [None]:
+            for peer in peers:
+                copy_z(f, peer, piece).start()
+
+    outer = [across(j) for j in range(near // 2)]
+    inner = [across(j) for j in range(near // 2, near)]
+    around = [beside(o) for o in range(near - 1, 0, -1)]
 
     def y_step(f, before):
-        for o in range(n_py - 1, 0, -1):
-            copy_y(f, o).wait_recv()
+        wait_lines(f)
         high, low = split(lines[f])
         for h in range(2):
             part = lax.rem(half + h + 1, 2)
             span = pl.ds(pl.multiple_of(part * half_rows, half_rows), half_rows)
             parts_out[f, span] = rows_transform(my[0, span], my[1, span], high, low)
             if h == 0:
-                for j in range(near // 2):
-                    copy_z(f, across(j)).start()
+                send_parts(f, outer)
                 if before is not None:
-                    send_second(before)
-                if f == fields - 1:
-                    send_second(f)
+                    send_parts(before, inner)
+                if f == last:
+                    send_parts(f, inner)
             else:
-                for o in range(near - 1, 0, -1):
-                    copy_z(f, beside(o)).start()
+                send_parts(f, around)
         parts[f, pl.ds(pz * rows_z, rows_z)] = parts_out[f, pl.ds(pz * rows_z, rows_z)]
 
     def relay():
@@ -277,16 +278,13 @@
         far_lines[pl.ds(py * rows_y, rows_y)] = far[py]
 
     def near_step():
-        for o in range(n_py - 1, 0, -1):
-            copy_y(0, o).wait_recv()
+        wait_lines(0)
         span = pl.ds(pl.multiple_of(half * half_rows, half_rows), half_rows)
         high, low = split(lines[0])
         parts_out[0, span] = rows_transform(my[0, span], my[1, span], high, low)
-        for o in range(near - 1, 0, -1):
-            copy_z(0, beside(o)).start()
+        send_parts(0, around)
         parts[0, pl.ds(pz * rows_z, rows_z)] = parts_out[0, pl.ds(pz * rows_z, rows_z)]
-        for o in range(n_py - 1, 0, -1):
-            copy_relay(o).wait_recv()
+        wait_for(far_lines.at[pl.ds(0, (n_py - 1) * rows_y)], recv_relay.at[0])
         high, low = split(far_lines[...])
         far_out[...] = rows_transform(my[0, span], my[1, span], high, low)
         for o in range(near - 1, 0, -1):
@@ -300,20 +298,25 @@
         if f == fields - 1:
             pl.when(raw_role)(near_step)
         if f == 1:
-            pl.when(plain_role)(functools.partial(send_second, 0))
+            pl.when(plain_role)(functools.partial(send_parts, 0, inner))
         y_step(f, f - 1 if f > 1 else None)
         if f == 1:
             pl.when(raw_role)(relay)
 
     row, col = iota((rows_out, nz), 0), iota((rows_out, nz), 1)
     pick = (row % nz == col).astype(F32).astype(BF16)
-    row, col = iota((nz, depth_z), 0), iota((nz, depth_z), 1)
-    spread = ((col // rows_z) * zl + col % zl == row).astype(F32).astype(BF16)
-    row, col = iota((rows_out, depth_z), 0), iota((rows_out, depth_z), 1)
-    keep = row // nz == (col // zl) % share_y
+    row, col = iota((nz, depth_g), 0), iota((nz, depth_g), 1)
+    spread = ((col // rows_g) * zl + col % zl == row).astype(F32).astype(BF16)
+    row, col = iota((rows_out, depth_g), 0), iota((rows_out, depth_g), 1)
+    keep = row // nz == (col // zl) % group
     for t in range(2):
         wide = dot(dot(pick, hz[t]).astype(BF16), spread)
         mz[t] = jnp.where(keep, wide, 0.0).astype(BF16)
+
+    def z_step(f, g):
+        starts = [p * rows_z + g * rows_g for p in range(n_pz)]
+        block = jnp.concatenate([parts[f, a : a + rows_g] for a in starts], axis=0)
+        return rows_transform(mz[0], mz[1], *split(block))
 
     diagonal = iota((nz, nz), 0) == iota((nz, nz), 1)
     sz_column = jnp.sum(jnp.where(diagonal, sz[...], 0.0), axis=1, keepdims=True)
@@ -322,24 +325,18 @@
         symbol = (sx_row + sy[pz * share_y + k]) + sz_column
         weights[pl.ds(k * nz, nz)] = 1.0 / (1.0 + symbol)
 
-    def wait_first(role):
-        for o in range(1, n_pz):
-            if o % 2 == 1 - role or o < near:
-                arrival_z(0, beside(o)).wait_recv()
-            if o % 2 == role and o < near:
-                copy_far(o).wait_recv()
-
-    last = fields - 1
+    def wait_parts(f, blocks):
+        wait_for(parts.at[f, pl.ds(0, blocks * rows_z)], recv_z.at[f])
+
     for f in [*range(1, last), 0, last]:
         if f == 0:
-            pl.when(raw_role)(functools.partial(wait_first, 0))
-            pl.when(plain_role)(functools.partial(wait_first, 1))
-        else:
-            for o in range(1, n_pz):
-                arrival_z(f, beside(o)).wait_recv()
-        high, low = split(parts[f])
+            pl.when(raw_role)(functools.partial(wait_parts, 0, n_pz - 2))
+            pl.when(plain_role)(functools.partial(wait_parts, 0, n_pz - 1))
+        elif f < last:
+            wait_parts(f, n_pz - 1)
         if f < last:
-            modes[f] = rows_transform(mz[0], mz[1], high, low)
+            for g in range(pieces):
+                modes[f, pl.ds(g * rows_out, rows_out)] = z_step(f, g)
         if f == 0:
             for k in range(share_y):
                 span = pl.ds(k * nz, nz)
@@ -352,31 +349,33 @@
                     mixed = (1.0 - weight) * mixed
                     out_ref[a, span] = mixed + weight * old[a] if a < last else mixed
         if f == last:
-            result = rows_transform(mz[0], mz[1], high, low)
-            weight = weights[...]
-            rest = (1.0 - weight) * result
-            for a in range(fields):
-                new = out_ref[a] + coupling[a, last] * rest
-                out_ref[a] = new + weight * result if a == last else new
+            for g in range(pieces):
+                wait_for(parts.at[f, pl.ds(0, (n_pz - 1) * rows_g)], recv_z.at[f + g])
+                span = pl.ds(g * rows_out, rows_out)
+                result = z_step(f, g)
+                weight = weights[span]
+                rest = (1.0 - weight) * result
+                for a in range(fields):
+                    new = out_ref[a, span] + coupling[a, last] * rest
+                    out_ref[a, span] = new + weight * result if a == last else new
+    def sent_parts(f, blocks):
+        wait_for(parts_out.at[f, pl.ds(0, blocks * rows_z)], send_z.at[f])
+
     for f in range(fields):
-        for o in range(1, n_py):
-            copy_y(f, o).wait_send()
-        for o in range(1, n_pz):
-            if f or o < near:
-                copy_z(f, beside(o)).wait_send()
+        wait_for(lines_out.at[f, pl.ds(0, n_py - 1)], send_y.at[f])
+        if f:
+            sent_parts(f, n_pz - 1)
 
     @pl.when(raw_role)
     def _():
         raw.wait_send()
-        for o in range(1, n_py):
-            copy_relay(o).wait_send()
-        for o in range(1, near):
-            copy_far(o).wait_send()
+        wait_for(far.at[pl.ds(0, n_py - 1)], send_relay.at[0])
+        wait_for(far_out.at[pl.ds(0, (near - 1) * rows_z)], send_far.at[0])
+        sent_parts(0, near - 1)
 
     @pl.when(plain_role)
     def _():
-        for o in range(near, n_pz):
-            copy_z(0, beside(o)).wait_send()
+        sent_parts(0, n_pz - 1)
 
 
 def shards(n_py, n_pz, species, coupling, symbol_x, symbol_y, symbol_z):
@@ -391,6 +390,7 @@
         return plain_shards(species, coupling, symbol_x, symbol_y, symbol_z)
     dims = (fields, ny, nz, n_py, n_pz, yl, zl, share_x, share_y)
     rows_y, depth_y, depth_z = yl * zl, ny * zl, share_y * nz
+    width = nz * max(g for g in range(1, share_y + 1) if share_y % g == 0 and g * nz <= max(nz, 256))
     vmem = pl.BlockSpec(memory_space=pltpu.VMEM)
     hbm = pl.BlockSpec(memory_space=pltpu.HBM)
     values = jnp.transpose(species, (0, 2, 3, 1)).reshape(fields, rows_y, nx)
@@ -415,22 +415,21 @@
             pltpu.VMEM((fields - 1, depth_z, share_x), F32),
             pltpu.VMEM((depth_z, share_x), F32),
             pltpu.VMEM((2, depth_y, depth_y), BF16),
-            pltpu.VMEM((2, depth_z, depth_z), BF16),
+            pltpu.VMEM((2, width, width), BF16),
             pltpu.VMEM((n_py, rows_y, share_x), F32),
             pltpu.VMEM((depth_y, share_x), F32),
             pltpu.VMEM((depth_y // 2, share_x), F32),
             pltpu.SemaphoreType.DMA((fields,)),
-            pltpu.SemaphoreType.DMA((8,)),
-            pltpu.SemaphoreType.DMA((fields, n_py)),
-            pltpu.SemaphoreType.DMA((fields, n_py)),
-            pltpu.SemaphoreType.DMA((fields, n_pz)),
-            pltpu.SemaphoreType.DMA((fields, n_pz)),
+            pltpu.SemaphoreType.DMA((7,)),
+            pltpu.SemaphoreType.DMA((fields,)),
+            pltpu.SemaphoreType.DMA((fields,)),
+            pltpu.SemaphoreType.DMA((fields,)),
+            pltpu.SemaphoreType.DMA((fields + share_y * nz // width - 1,)),
             pltpu.SemaphoreType.DMA((1,)),
             pltpu.SemaphoreType.DMA((1,)),
-            pltpu.SemaphoreType.DMA((n_py,)),
-            pltpu.SemaphoreType.DMA((n_py,)),
-            pltpu.SemaphoreType.DMA((n_pz // 2,)),
-            pltpu.SemaphoreType.DMA((n_pz // 2,)),
+            pltpu.SemaphoreType.DMA((1,)),
+            pltpu.SemaphoreType.DMA((1,)),
+            pltpu.SemaphoreType.DMA((1,)),
         ],
         compiler_params=pltpu.CompilerParams(
             collective_id=0, has_side_effects=True, vmem_limit_bytes=54500000

time: 34 us -> 32.7 us (0.962)
  Pallas kernels: 32.9 us -> 31.6 us
    pallas_call x1, Pallas kernels: 32.9 us -> 31.6 us  [shards(): pl.pallas_call(functools.partial(kernel, dims), out_shape=jax.ShapeDtypeS...]
where the time goes in v3:
time: 32.7 us; the launch traced here: 32.6 us
  Pallas kernels  31.6 us (97%)
  local copies, waits for them, and re-layouts  0.97 us (3%)
    pallas_call x1, Pallas kernels, shards(): pl.pallas_call(functools.partial(kernel, dims), out_shape=jax.ShapeDtypeS...  31.6 us
    unnamed x1, local copies, waits for them, and re-layouts  0.97 us

profile of v3, /device:TPU:9, one launch (start us, length us, event | category | flops | bytes accessed | tf_op | source)
XLA Modules:
  0.0 32.6 jit_solution(12073713359342372566)
XLA Ops:
  0.0 31.6 %shard_map.82 = f32[4,512,128]{2,1,0:T(8,128)S(1)} custom-call(f32[4,128,512]{2,1,0:T(8,128)} %bitcast.9, bf16[2,512,512]{2,1,0:T(8,128)(2,1)} %constant.4.clone.hx_hbm, bf16[2,64,64]{2,1,0:T(8,128)(2,1)} %constant.5.clone.hy_hbm.hz_hbm, bf16[2,64,64]{2,1,0:T(8,128)(2,1)} %constant.5.clone.hy_hbm.hz_hbm, f32[4,4]{1,0:T(4,128)} %coupling_hbm.1, ...), custom_call_target="tpu_custom_call" | custom-call | tf_op jit(solution)/shard_map/pallas_call | solution.py:397
  31.6 1.0 %copy.10 = f32[4,128,8,64]{1,3,2,0:T(8,128)} copy(f32[4,128,8,64]{1,3,2,0:T(8,128)S(1)} %bitcast.8) | data formatting | bytes 2097152

commit v4 on v3

--- a/solution.py
+++ b/solution.py
@@ -13,6 +13,7 @@
 BF16 = jnp.bfloat16
 LANES, SUBLANES = 128, 8
 VMEM_BUDGET = 48 << 20
+RAW_SHARES = ((0, 1, 2), (0, 1, 3))
 
 
 def mode_table(count):
@@ -164,24 +165,43 @@
         wait_for(lines.at[f, pl.ds(0, (n_py - 1) * rows_y)], recv_y.at[f])
 
     mirror = flipped(pz, near, n_pz)
-    raw_role = lax.rem(pz, 2) == 0
+    early = lax.rem(pz, 2) == 0
+    pair = lax.rem(pz // 2, 2)
+
+    def is_raw(share):
+        found = jnp.bool_(False)
+        for bit, shares in enumerate(RAW_SHARES):
+            for s in shares:
+                found = found | ((pair == bit) & (share == s))
+        return early & found
+
+    raw_role = is_raw(py)
     plain_role = jnp.logical_not(raw_role)
 
-    raw = pltpu.make_async_remote_copy(
-        src_ref=lines_out.at[0],
-        dst_ref=far,
-        send_sem=send_raw.at[0],
-        recv_sem=recv_raw.at[0],
-        device_id={"pz": mirror},
-        device_id_type=MESH,
-    )
+    def each_pair(do):
+        for bit, shares in enumerate(RAW_SHARES):
+            pl.when(early & (pair == bit))(functools.partial(do, shares))
+
+    def copy_raw(share):
+        return pltpu.make_async_remote_copy(
+            src_ref=lines_out.at[0, share],
+            dst_ref=far.at[share],
+            send_sem=send_raw.at[0],
+            recv_sem=recv_raw.at[0],
+            device_id={"pz": mirror},
+            device_id_type=MESH,
+        )
+
+    def send_raws(shares):
+        for share in shares:
+            copy_raw(share).start()
 
     def copy_relay(o):
         to = flipped(py, o, n_py)
         return pltpu.make_async_remote_copy(
             src_ref=far.at[to],
             dst_ref=far_lines.at[pl.ds(py * rows_y, rows_y)],
-            send_sem=send_relay.at[0],
+            send_sem=send_relay.at[o],
             recv_sem=recv_relay.at[0],
             device_id={"py": to},
             device_id_type=MESH,
@@ -207,18 +227,25 @@
         result = both[:rows_y] + both[rows_y:] + dot(high, hx[1])
         for d in range(n_py):
             lines_out[f, d] = result[:, d * share_x : (d + 1) * share_x]
-        def send_lines(f):
+        def send_lines(f, when=None):
             for o in range(n_py - 1, 0, -1):
-                copy_y(f, o).start()
+                start = copy_y(f, o).start
+                if when is None:
+                    start()
+                else:
+                    pl.when(is_raw(flipped(py, o, n_py)) == when)(start)
 
         if f == 0:
             pl.semaphore_wait(barrier, n_py + n_pz - 2)
-            pl.when(raw_role)(raw.start)
-            pl.when(plain_role)(functools.partial(send_lines, 0))
+            each_pair(send_raws)
+            send_lines(0, False)
+        elif f == 1:
+            pl.when(jnp.logical_not(early))(functools.partial(send_lines, 1))
         else:
+            if f == 2:
+                pl.when(early)(functools.partial(send_lines, 1))
+                send_lines(0, True)
             send_lines(f)
-        if f == 1:
-            pl.when(raw_role)(functools.partial(send_lines, 0))
         lines[f, pl.ds(py * rows_y, rows_y)] = lines_out[f, py]
 
     for side in sides[1:]:
@@ -272,10 +299,13 @@
         parts[f, pl.ds(pz * rows_z, rows_z)] = parts_out[f, pl.ds(pz * rows_z, rows_z)]
 
     def relay():
-        raw.wait_recv()
+        each_pair(lambda shares: wait_for(far.at[pl.ds(0, len(shares))], recv_raw.at[0]))
         for o in range(n_py - 1, 0, -1):
-            copy_relay(o).start()
-        far_lines[pl.ds(py * rows_y, rows_y)] = far[py]
+            pl.when(is_raw(flipped(py, o, n_py)))(copy_relay(o).start)
+
+        @pl.when(raw_role)
+        def _():
+            far_lines[pl.ds(py * rows_y, rows_y)] = far[py]
 
     def near_step():
         wait_lines(0)
@@ -301,7 +331,7 @@
             pl.when(plain_role)(functools.partial(send_parts, 0, inner))
         y_step(f, f - 1 if f > 1 else None)
         if f == 1:
-            pl.when(raw_role)(relay)
+            relay()
 
     row, col = iota((rows_out, nz), 0), iota((rows_out, nz), 1)
     pick = (row % nz == col).astype(F32).astype(BF16)
@@ -366,10 +396,12 @@
         if f:
             sent_parts(f, n_pz - 1)
 
+    each_pair(lambda shares: wait_for(far.at[pl.ds(0, len(shares))], send_raw.at[0]))
+    for o in range(1, n_py):
+        pl.when(is_raw(flipped(py, o, n_py)))(copy_relay(o).wait_send)
+
     @pl.when(raw_role)
     def _():
-        raw.wait_send()
-        wait_for(far.at[pl.ds(0, n_py - 1)], send_relay.at[0])
         wait_for(far_out.at[pl.ds(0, (near - 1) * rows_z)], send_far.at[0])
         sent_parts(0, near - 1)
 
@@ -427,7 +459,7 @@
             pltpu.SemaphoreType.DMA((fields + share_y * nz // width - 1,)),
             pltpu.SemaphoreType.DMA((1,)),
             pltpu.SemaphoreType.DMA((1,)),
-            pltpu.SemaphoreType.DMA((1,)),
+            pltpu.SemaphoreType.DMA((n_py,)),
             pltpu.SemaphoreType.DMA((1,)),
             pltpu.SemaphoreType.DMA((1,)),
         ],

time: 32.7 us -> 32.3 us (0.988)
  the two profiles are of different devices: /device:TPU:9 before, /device:TPU:15 now
where the time goes in v4:
time: 32.3 us; the launch traced here: 32.1 us
  Pallas kernels  31.1 us (96%)
  local copies, waits for them, and re-layouts  0.97 us (3%)
    pallas_call x1, Pallas kernels, shards(): pl.pallas_call(functools.partial(kernel, dims), out_shape=jax.ShapeDtypeS...  31.1 us
    unnamed x1, local copies, waits for them, and re-layouts  0.97 us

profile of v4, /device:TPU:15, one launch (start us, length us, event | category | flops | bytes accessed | tf_op | source)
XLA Modules:
  0.0 32.1 jit_solution(12634460855049678698)
XLA Ops:
  0.0 31.1 %shard_map.82 = f32[4,512,128]{2,1,0:T(8,128)S(1)} custom-call(f32[4,128,512]{2,1,0:T(8,128)} %bitcast.9, bf16[2,512,512]{2,1,0:T(8,128)(2,1)} %constant.4.clone.hx_hbm, bf16[2,64,64]{2,1,0:T(8,128)(2,1)} %constant.5.clone.hy_hbm.hz_hbm, bf16[2,64,64]{2,1,0:T(8,128)(2,1)} %constant.5.clone.hy_hbm.hz_hbm, f32[4,4]{1,0:T(4,128)} %coupling_hbm.1, ...), custom_call_target="tpu_custom_call" | custom-call | tf_op jit(solution)/shard_map/pallas_call | solution.py:429
  31.1 1.0 %copy.10 = f32[4,128,8,64]{1,3,2,0:T(8,128)} copy(f32[4,128,8,64]{1,3,2,0:T(8,128)S(1)} %bitcast.8) | data formatting | bytes 2097152

commit v5 on v4

--- a/solution.py
+++ b/solution.py
@@ -13,7 +13,7 @@
 BF16 = jnp.bfloat16
 LANES, SUBLANES = 128, 8
 VMEM_BUDGET = 48 << 20
-RAW_SHARES = ((0, 1, 2), (0, 1, 3))
+RAW_SHARES = ((0, 1, 3), (0, 2))
 
 
 def mode_table(count):
@@ -105,7 +105,7 @@
         return pltpu.make_async_copy(field_ref.at[f], held.at[f], load_sem.at[f])
 
     pairs = (
-        (hx_hbm, hx), (hy_hbm, hy), (hz_hbm, hz),
+        (hx_hbm.at[0], hx.at[0]), (hx_hbm.at[1], hx.at[1]), (hy_hbm, hy), (hz_hbm, hz),
         (coupling_hbm, coupling), (sx_hbm, sx), (sy_hbm, sy), (sz_hbm, sz),
     )
     sides = [
@@ -122,10 +122,7 @@
         )
     load(0).start()
     sides[0].start()
-    for f in range(1, fields):
-        load(f).start()
-    for side in sides[1:]:
-        side.start()
+    sides[1].start()
 
     def copy_y(f, o):
         to = flipped(py, o, n_py)
@@ -223,12 +220,18 @@
         high, low = split(held[f])
         if f == 0:
             sides[0].wait()
+            for later in range(1, fields):
+                load(later).start()
+            for side in sides[2:]:
+                side.start()
         both = dot(jnp.concatenate([high, low], axis=0), hx[0])
+        if f == 0:
+            sides[1].wait()
         result = both[:rows_y] + both[rows_y:] + dot(high, hx[1])
         for d in range(n_py):
             lines_out[f, d] = result[:, d * share_x : (d + 1) * share_x]
         def send_lines(f, when=None):
-            for o in range(n_py - 1, 0, -1):
+            for o in (1, 2, 3):
                 start = copy_y(f, o).start
                 if when is None:
                     start()
@@ -238,8 +241,9 @@
         if f == 0:
             pl.semaphore_wait(barrier, n_py + n_pz - 2)
             each_pair(send_raws)
-            send_lines(0, False)
+            pl.when(jnp.logical_not(early))(functools.partial(send_lines, 0))
         elif f == 1:
+            pl.when(early)(functools.partial(send_lines, 0, False))
             pl.when(jnp.logical_not(early))(functools.partial(send_lines, 1))
         else:
             if f == 2:
@@ -248,7 +252,7 @@
             send_lines(f)
         lines[f, pl.ds(py * rows_y, rows_y)] = lines_out[f, py]
 
-    for side in sides[1:]:
+    for side in sides[2:]:
         side.wait()
 
     def iota(shape, dim):
@@ -277,6 +281,7 @@
             for peer in peers:
                 copy_z(f, peer, piece).start()
 
+    deep = lax.rem(pz // (near // 2), 2) == half
     outer = [across(j) for j in range(near // 2)]
     inner = [across(j) for j in range(near // 2, near)]
     around = [beside(o) for o in range(near - 1, 0, -1)]
@@ -284,18 +289,23 @@
     def y_step(f, before):
         wait_lines(f)
         high, low = split(lines[f])
-        for h in range(2):
-            part = lax.rem(half + h + 1, 2)
-            span = pl.ds(pl.multiple_of(part * half_rows, half_rows), half_rows)
+        def transform(first, rows):
+            span = pl.ds(pl.multiple_of(first, rows), rows)
             parts_out[f, span] = rows_transform(my[0, span], my[1, span], high, low)
-            if h == 0:
-                send_parts(f, outer)
-                if before is not None:
-                    send_parts(before, inner)
-                if f == last:
-                    send_parts(f, inner)
-            else:
-                send_parts(f, around)
+
+        quarter = half_rows // 2
+        far_half = (1 - half) * half_rows
+        transform(far_half + (1 - half) * quarter, quarter)
+        send_parts(f, outer)
+        transform(far_half + half * quarter, quarter)
+        if before is not None:
+            pl.when(jnp.logical_not(deep))(functools.partial(send_parts, before, inner))
+        if f == last:
+            send_parts(f, inner)
+        else:
+            pl.when(deep)(functools.partial(send_parts, f, inner))
+        transform(half * half_rows, half_rows)
+        send_parts(f, around)
         parts[f, pl.ds(pz * rows_z, rows_z)] = parts_out[f, pl.ds(pz * rows_z, rows_z)]
 
     def relay():
@@ -328,7 +338,7 @@
         if f == fields - 1:
             pl.when(raw_role)(near_step)
         if f == 1:
-            pl.when(plain_role)(functools.partial(send_parts, 0, inner))
+            pl.when(plain_role & jnp.logical_not(deep))(functools.partial(send_parts, 0, inner))
         y_step(f, f - 1 if f > 1 else None)
         if f == 1:
             relay()
@@ -452,7 +462,7 @@
             pltpu.VMEM((depth_y, share_x), F32),
             pltpu.VMEM((depth_y // 2, share_x), F32),
             pltpu.SemaphoreType.DMA((fields,)),
-            pltpu.SemaphoreType.DMA((7,)),
+            pltpu.SemaphoreType.DMA((8,)),
             pltpu.SemaphoreType.DMA((fields,)),
             pltpu.SemaphoreType.DMA((fields,)),
             pltpu.SemaphoreType.DMA((fields,)),

time: 32.3 us -> 31.7 us (0.981)
  the two profiles are of different devices: /device:TPU:15 before, /device:TPU:18 now
where the time goes in v5:
time: 31.7 us; the launch traced here: 31.5 us
  Pallas kernels  30.5 us (96%)
  local copies, waits for them, and re-layouts  0.97 us (3%)
    pallas_call x1, Pallas kernels, shards(): pl.pallas_call(functools.partial(kernel, dims), out_shape=jax.ShapeDtypeS...  30.5 us
    unnamed x1, local copies, waits for them, and re-layouts  0.97 us

profile of v5, /device:TPU:18, one launch (start us, length us, event | category | flops | bytes accessed | tf_op | source)
XLA Modules:
  0.0 31.5 jit_solution(15573922369232366849)
XLA Ops:
  0.0 30.5 %shard_map.82 = f32[4,512,128]{2,1,0:T(8,128)S(1)} custom-call(f32[4,128,512]{2,1,0:T(8,128)} %bitcast.9, bf16[2,512,512]{2,1,0:T(8,128)(2,1)} %constant.4.clone.hx_hbm, bf16[2,64,64]{2,1,0:T(8,128)(2,1)} %constant.5.clone.hy_hbm.hz_hbm, bf16[2,64,64]{2,1,0:T(8,128)(2,1)} %constant.5.clone.hy_hbm.hz_hbm, f32[4,4]{1,0:T(4,128)} %coupling_hbm.1, ...), custom_call_target="tpu_custom_call" | custom-call | tf_op jit(solution)/shard_map/pallas_call | solution.py:439
  30.5 1.0 %copy.10 = f32[4,128,8,64]{1,3,2,0:T(8,128)} copy(f32[4,128,8,64]{1,3,2,0:T(8,128)S(1)} %bitcast.8) | data formatting | bytes 2097152

commit v6 on v5

--- a/solution.py
+++ b/solution.py
@@ -13,7 +13,6 @@
 BF16 = jnp.bfloat16
 LANES, SUBLANES = 128, 8
 VMEM_BUDGET = 48 << 20
-RAW_SHARES = ((0, 1, 3), (0, 2))
 
 
 def mode_table(count):
@@ -165,9 +164,11 @@
     early = lax.rem(pz, 2) == 0
     pair = lax.rem(pz // 2, 2)
 
+    raw_shares = (tuple(range(0, n_py, 2)), (0, *range(1, n_py, 2)))
+
     def is_raw(share):
         found = jnp.bool_(False)
-        for bit, shares in enumerate(RAW_SHARES):
+        for bit, shares in enumerate(raw_shares):
             for s in shares:
                 found = found | ((pair == bit) & (share == s))
         return early & found
@@ -176,7 +177,7 @@
     plain_role = jnp.logical_not(raw_role)
 
     def each_pair(do):
-        for bit, shares in enumerate(RAW_SHARES):
+        for bit, shares in enumerate(raw_shares):
             pl.when(early & (pair == bit))(functools.partial(do, shares))
 
     def copy_raw(share):
@@ -214,6 +215,17 @@
             device_id={"pz": to},
             device_id_type=MESH,
         )
+
+    last = fields - 1
+    late_role = jnp.logical_not(early)
+
+    def send_lines(f, when=None):
+        for o in range(1, n_py):
+            start = copy_y(f, o).start
+            if when is None:
+                start()
+            else:
+                pl.when(is_raw(flipped(py, o, n_py)) == when)(start)
 
     for f in range(fields):
         load(f).wait()
@@ -230,26 +242,19 @@
         result = both[:rows_y] + both[rows_y:] + dot(high, hx[1])
         for d in range(n_py):
             lines_out[f, d] = result[:, d * share_x : (d + 1) * share_x]
-        def send_lines(f, when=None):
-            for o in (1, 2, 3):
-                start = copy_y(f, o).start
-                if when is None:
-                    start()
-                else:
-                    pl.when(is_raw(flipped(py, o, n_py)) == when)(start)
-
         if f == 0:
             pl.semaphore_wait(barrier, n_py + n_pz - 2)
             each_pair(send_raws)
-            pl.when(jnp.logical_not(early))(functools.partial(send_lines, 0))
-        elif f == 1:
-            pl.when(early)(functools.partial(send_lines, 0, False))
-            pl.when(jnp.logical_not(early))(functools.partial(send_lines, 1))
+            pl.when(late_role)(functools.partial(send_lines, 0))
+        elif f < last:
+            if f == 1:
+                pl.when(early)(functools.partial(send_lines, 0, False))
+            pl.when(late_role)(functools.partial(send_lines, f))
         else:
-            if f == 2:
-                pl.when(early)(functools.partial(send_lines, 1))
-                send_lines(0, True)
-            send_lines(f)
+            for held_back in range(1, last):
+                pl.when(early)(functools.partial(send_lines, held_back))
+            send_lines(0, True)
+            send_lines(last)
         lines[f, pl.ds(py * rows_y, rows_y)] = lines_out[f, py]
 
     for side in sides[2:]:
@@ -273,7 +278,6 @@
 
     half_rows = depth_y // 2
 
-    last = fields - 1
     pieces = share_y // group
 
     def send_parts(f, peers):

time: 31.7 us -> 31.4 us (level)
  the two profiles are of different devices: /device:TPU:18 before, /device:TPU:9 now
where the time goes in v6:
time: 31.4 us; the launch traced here: 30.8 us
  Pallas kernels  29.8 us (95%)
  local copies, waits for them, and re-layouts  0.97 us (3%)
    pallas_call x1, Pallas kernels, shards(): pl.pallas_call(functools.partial(kernel, dims), out_shape=jax.ShapeDtypeS...  29.8 us
    unnamed x1, local copies, waits for them, and re-layouts  0.97 us

profile of v6, /device:TPU:9, one launch (start us, length us, event | category | flops | bytes accessed | tf_op | source)
XLA Modules:
  0.0 30.8 jit_solution(13011411615222332839)
XLA Ops:
  0.0 29.8 %shard_map.82 = f32[4,512,128]{2,1,0:T(8,128)S(1)} custom-call(f32[4,128,512]{2,1,0:T(8,128)} %bitcast.9, bf16[2,512,512]{2,1,0:T(8,128)(2,1)} %constant.4.clone.hx_hbm, bf16[2,64,64]{2,1,0:T(8,128)(2,1)} %constant.5.clone.hy_hbm.hz_hbm, bf16[2,64,64]{2,1,0:T(8,128)(2,1)} %constant.5.clone.hy_hbm.hz_hbm, f32[4,4]{1,0:T(4,128)} %coupling_hbm.1, ...), custom_call_target="tpu_custom_call" | custom-call | tf_op jit(solution)/shard_map/pallas_call | solution.py:443
  29.8 1.0 %copy.10 = f32[4,128,8,64]{1,3,2,0:T(8,128)} copy(f32[4,128,8,64]{1,3,2,0:T(8,128)S(1)} %bitcast.8) | data formatting | bytes 2097152

commit v7 on v6

--- a/solution.py
+++ b/solution.py
@@ -129,7 +129,7 @@
             src_ref=lines_out.at[f, to],
             dst_ref=lines.at[f, pl.ds(py * rows_y, rows_y)],
             send_sem=send_y.at[f],
-            recv_sem=recv_y.at[f],
+            recv_sem=recv_y.at[fields if f == 0 and o == n_py - 1 else f],
             device_id={"py": to},
             device_id_type=MESH,
         )
@@ -158,7 +158,10 @@
         pltpu.make_async_copy(ref, ref, sem).wait()
 
     def wait_lines(f):
-        wait_for(lines.at[f, pl.ds(0, (n_py - 1) * rows_y)], recv_y.at[f])
+        blocks = n_py - 1 if f else n_py - 2
+        wait_for(lines.at[f, pl.ds(0, blocks * rows_y)], recv_y.at[f])
+        if f == 0:
+            wait_for(lines.at[f, pl.ds(0, rows_y)], recv_y.at[fields])
 
     mirror = flipped(pz, near, n_pz)
     early = lax.rem(pz, 2) == 0
@@ -290,17 +293,40 @@
     inner = [across(j) for j in range(near // 2, near)]
     around = [beside(o) for o in range(near - 1, 0, -1)]
 
+    def first_quarter(first, rows):
+        wait_for(lines.at[0, pl.ds(0, (n_py - 2) * rows_y)], recv_y.at[0])
+        span = pl.ds(pl.multiple_of(first, rows), rows)
+
+        def partial(offsets):
+            starts = [pl.multiple_of(flipped(py, o, n_py) * rows_y, rows_y) for o in offsets]
+            block = jnp.concatenate([lines[0, pl.ds(a, rows_y)] for a in starts], axis=0)
+            tables = [
+                jnp.concatenate([my[t, span, pl.ds(a, rows_y)] for a in starts], axis=1)
+                for t in range(2)
+            ]
+            return rows_transform(tables[0], tables[1], *split(block))
+
+        near_sum = partial(range(n_py - 1))
+        wait_for(lines.at[0, pl.ds(0, rows_y)], recv_y.at[fields])
+        parts_out[0, span] = near_sum + partial([n_py - 1])
+
     def y_step(f, before):
-        wait_lines(f)
+        quarter = half_rows // 2
+        far_half = (1 - half) * half_rows
+        if f:
+            wait_lines(f)
+        else:
+            first_quarter(far_half + (1 - half) * quarter, quarter)
+            send_parts(f, outer)
         high, low = split(lines[f])
+
         def transform(first, rows):
             span = pl.ds(pl.multiple_of(first, rows), rows)
             parts_out[f, span] = rows_transform(my[0, span], my[1, span], high, low)
 
-        quarter = half_rows // 2
-        far_half = (1 - half) * half_rows
-        transform(far_half + (1 - half) * quarter, quarter)
-        send_parts(f, outer)
+        if f:
+            transform(far_half + (1 - half) * quarter, quarter)
+            send_parts(f, outer)
         transform(far_half + half * quarter, quarter)
         if before is not None:
             pl.when(jnp.logical_not(deep))(functools.partial(send_parts, before, inner))
@@ -468,7 +494,7 @@
             pltpu.SemaphoreType.DMA((fields,)),
             pltpu.SemaphoreType.DMA((8,)),
             pltpu.SemaphoreType.DMA((fields,)),
-            pltpu.SemaphoreType.DMA((fields,)),
+            pltpu.SemaphoreType.DMA((fields + 1,)),
             pltpu.SemaphoreType.DMA((fields,)),
             pltpu.SemaphoreType.DMA((fields + share_y * nz // width - 1,)),
             pltpu.SemaphoreType.DMA((1,)),

time: 31.4 us -> 31.4 us (level)
  no operation moved by 1% of the time
where the time goes in v7:
time: 31.4 us; the launch traced here: 30.8 us
  Pallas kernels  29.8 us (95%)
  local copies, waits for them, and re-layouts  0.97 us (3%)
    pallas_call x1, Pallas kernels, shards(): pl.pallas_call(functools.partial(kernel, dims), out_shape=jax.ShapeDtypeS...  29.8 us
    unnamed x1, local copies, waits for them, and re-layouts  0.97 us

profile of v7, /device:TPU:9, one launch (start us, length us, event | category | flops | bytes accessed | tf_op | source)
XLA Modules:
  0.0 30.8 jit_solution(1311190156818711191)
XLA Ops:
  0.0 29.8 %shard_map.82 = f32[4,512,128]{2,1,0:T(8,128)S(1)} custom-call(f32[4,128,512]{2,1,0:T(8,128)} %bitcast.9, bf16[2,512,512]{2,1,0:T(8,128)(2,1)} %constant.4.clone.hx_hbm, bf16[2,64,64]{2,1,0:T(8,128)(2,1)} %constant.5.clone.hy_hbm.hz_hbm, bf16[2,64,64]{2,1,0:T(8,128)(2,1)} %constant.5.clone.hy_hbm.hz_hbm, f32[4,4]{1,0:T(4,128)} %coupling_hbm.1, ...), custom_call_target="tpu_custom_call" | custom-call | tf_op jit(solution)/shard_map/pallas_call | solution.py:469
  29.8 1.0 %copy.10 = f32[4,128,8,64]{1,3,2,0:T(8,128)} copy(f32[4,128,8,64]{1,3,2,0:T(8,128)S(1)} %bitcast.8) | data formatting | bytes 2097152
